TPU v7x, 32 devices: a whole 2x2x4 slice. The times are simulated.
32 devices in a mesh: row: 4 (over z), col: 2 (over x), depth: 4 (over y, core).
Axes of the slice: x: 2, y: 2, z: 4, core: 2. Of those that a mesh axis runs over, the one named last changes fastest.
Arguments:
- pair_input: bfloat16 [192, 192, 128], P('row', ('col', 'depth')), may hold values from -40 to 40
- in_gain: float32 [128], replicated, may hold values from 0.1 to 1.9
- in_shift: float32 [128], replicated, may hold values from -3 to 3
- w_proj: bfloat16 [128, 512], replicated, may hold values from -0.5 to 0.5
- w_gate: bfloat16 [128, 128], replicated, may hold values from -0.5 to 0.5
- out_gain: float32 [128], replicated, may hold values from 0.1 to 1.9
- out_shift: float32 [128], replicated, may hold values from -3 to 3
- w_out: bfloat16 [128, 128], replicated, may hold values from -0.5 to 0.5
Outputs:
- update: bfloat16 [192, 192, 128], P('row', ('col', 'depth'))
All inputs are finite; a program needn't handle non-finite values.
Results may differ from a plain program's by a relative error of at most 0.013.
Values may be sent and summed in bfloat16 or wider, within the bound.
A program may use at most 64 MiB of HBM per device.

v0:
```python
import jax
import jax.numpy as jnp
from jax import lax
from jax.sharding import PartitionSpec as P


def layer_norm(values, scaling, offsets):
    average = jnp.mean(values, axis=-1, keepdims=True)
    centred = values - average
    variance = jnp.mean(centred * centred, axis=-1, keepdims=True)
    return centred * lax.rsqrt(variance + 1e-05) * scaling + offsets


def gated_sides(normed, w_proj):
    channels = w_proj.shape[1] // 4
    projected = jnp.einsum("xyc,cd->xyd", normed, w_proj, preferred_element_type=jnp.float32)
    left_side = (
        jax.nn.sigmoid(projected[..., :channels]) * projected[..., channels : 2 * channels]
    ).astype(jnp.bfloat16)
    right_side = (
        jax.nn.sigmoid(projected[..., 2 * channels : 3 * channels]) * projected[..., 3 * channels :]
    ).astype(jnp.bfloat16)
    return (left_side, right_side)


def reorder_channels(values, row_count, other_count):
    shape_rest = values.shape[1:]
    grouped = values.reshape((row_count, other_count, -1) + shape_rest)
    return jnp.swapaxes(grouped, 0, 1).reshape(values.shape)


def per_device(pair_input, in_gain, in_shift, w_proj, w_gate, out_gain, out_shift, w_out):
    row_count = lax.axis_size("row")
    col_count = lax.axis_size("col")
    depth_count = lax.axis_size("depth")
    normed = layer_norm(pair_input.astype(jnp.float32), in_gain, in_shift).astype(jnp.bfloat16)
    left_side, right_side = gated_sides(normed, w_proj)
    left_all, right_all = (
        lax.all_to_all(
            lax.all_to_all(left_side, "row", split_axis=2, concat_axis=0, tiled=True),
            ("col", "depth"),
            split_axis=2,
            concat_axis=1,
            tiled=True,
        ),
        lax.all_to_all(
            lax.all_to_all(right_side, "row", split_axis=2, concat_axis=0, tiled=True),
            ("col", "depth"),
            split_axis=2,
            concat_axis=1,
            tiled=True,
        ),
    )
    planes = jnp.einsum("kic,kjc->ijc", left_all, right_all, preferred_element_type=jnp.float32)
    product = lax.all_to_all(
        lax.all_to_all(planes.astype(jnp.bfloat16), "row", split_axis=0, concat_axis=2, tiled=True),
        ("col", "depth"),
        split_axis=1,
        concat_axis=2,
        tiled=True,
    ).astype(planes.dtype)
    other_count = col_count * depth_count
    used_gain = reorder_channels(out_gain, row_count, other_count)
    used_shift = reorder_channels(out_shift, row_count, other_count)
    used_out = reorder_channels(w_out, row_count, other_count)
    product_norm = layer_norm(product, used_gain, used_shift).astype(jnp.bfloat16)
    gating = jax.nn.sigmoid(
        jnp.einsum("xyc,cd->xyd", normed, w_gate, preferred_element_type=jnp.float32)
    )
    projected_out = jnp.einsum(
        "xyc,cd->xyd", product_norm, used_out, preferred_element_type=jnp.float32
    )
    return (gating * projected_out).astype(jnp.bfloat16)


def solution(mesh):
    placed = (P("row", ("col", "depth"), None), P(), P(), P(), P(), P(), P(), P())
    return jax.shard_map(
        per_device,
        mesh=mesh,
        in_specs=placed,
        out_specs=P("row", ("col", "depth"), None),
        check_vma=False,
    )
```

profile of v0, /device:TPU:0, one launch (start us, length us, event | category | flops | bytes accessed | tf_op | source)
XLA Modules:
  0.0 87.3 jit_solution(1574282504677348500)
XLA Ops:
  0.0 1.2 %convert_reduce_fusion = f32[48,24]{1,0:T(8,128)S(1)} fusion(bf16[48,24,128]{2,1,0:T(8,128)(2,1)} %param.8), kind=kLoop, calls=%fused_computation.18 | loop fusion | flops 293760 | bytes 299520 | tf_op jit(solution)/shard_map/reduce_sum | solution.py:8
  1.4 1.4 %fusion.15 = f32[48,24]{1,0:T(8,128)S(1)} fusion(bf16[48,24,128]{2,1,0:T(8,128)(2,1)} %param.8, f32[48,24]{1,0:T(8,128)S(1)} %copy.86), kind=kLoop, calls=%fused_computation.21 | loop fusion | flops 588672 | bytes 304128 | tf_op jit(solution)/shard_map/reduce_sum | solution.py:10
  2.9 1.6 %fusion.27 = f32[48,24,512]{2,1,0:T(8,128)S(1)} fusion(bf16[128,512]{1,0:T(8,128)(2,1)S(1)} %copy-done, bf16[48,24,128]{2,1,0:T(8,128)(2,1)} %param.8, f32[128]{0:T(128)} %param.10, f32[128]{0:T(128)} %param.9, f32[48,24]{1,0:T(8,128)S(1)} %copy.88, f32[48,24]{1,0:T(8,128)S(1)} %copy.86), kind=kOutput, calls=%fused_computation.37 | convolution fusion | flops 151879680 | bytes 2795520 | tf_op jit(solution)/shard_map/xyc,cd->xyd/dot_general | solution.py:16
  5.3 2.0 %reshape.59 = bf16[4,2,18432]{2,1,0:T(2,128)(2,1)} reshape(bf16[128,24,48]{2,1,0:T(8,128)(2,1)S(1)} %bitcast.78) | data formatting | bytes 589824
  7.3 6.3 %all-to-all-start.2 = ((bf16[4,2,18432]{2,1,0:T(2,128)(2,1)}), bf16[4,2,18432]{2,1,0:T(2,128)(2,1)S(1)}, u32[]{:S(2)}, u32[]{:S(2)}) async-start(bf16[4,2,18432]{2,1,0:T(2,128)(2,1)} %reshape.59), calls=%async_computation.2 | async-start | bytes 589824 | tf_op jit(solution)/shard_map/all_to_all | solution.py:40
  14.1 2.0 %reshape.57 = bf16[4,2,18432]{2,1,0:T(2,128)(2,1)} reshape(bf16[128,24,48]{2,1,0:T(8,128)(2,1)S(1)} %bitcast.79) | data formatting | bytes 589824
  16.2 7.1 %all-to-all-done.2 = bf16[4,2,18432]{2,1,0:T(2,128)(2,1)S(1)} async-done(((bf16[4,2,18432]{2,1,0:T(2,128)(2,1)}), bf16[4,2,18432]{2,1,0:T(2,128)(2,1)S(1)}, u32[]{:S(2)}, u32[]{:S(2)}) %all-to-all-start.2) | async-done | bytes 294944 | tf_op jit(solution)/shard_map/all_to_all | solution.py:40
  23.3 3.5 %all-to-all-start = ((bf16[4,2,18432]{2,1,0:T(2,128)(2,1)}), bf16[4,2,18432]{2,1,0:T(2,128)(2,1)S(1)}, u32[]{:S(2)}, u32[]{:S(2)}) async-start(bf16[4,2,18432]{2,1,0:T(2,128)(2,1)} %reshape.57), calls=%async_computation | async-start | bytes 589824 | tf_op jit(solution)/shard_map/all_to_all | solution.py:47
  26.7 0.8 reshape.60
  28.1 1.2 %reshape.56 = bf16[192,24,32]{0,1,2:T(8,128)(2,1)} reshape(bf16[4,48,24,32]{1,0,2,3:T(4,128)(2,1)S(1)} %copy.115) | data formatting | bytes 589824 | tf_op jit(solution)/shard_map/all_to_all | solution.py:40
  29.3 5.5 %all-to-all-done = bf16[4,2,18432]{2,1,0:T(2,128)(2,1)S(1)} async-done(((bf16[4,2,18432]{2,1,0:T(2,128)(2,1)}), bf16[4,2,18432]{2,1,0:T(2,128)(2,1)S(1)}, u32[]{:S(2)}, u32[]{:S(2)}) %all-to-all-start) | async-done | bytes 294944 | tf_op jit(solution)/shard_map/all_to_all | solution.py:47
  34.9 3.7 %all-to-all-start.3 = ((bf16[192,24,32]{0,1,2:T(8,128)(2,1)}), bf16[192,24,32]{0,1,2:T(8,128)(2,1)S(1)}, u32[]{:S(2)}, u32[]{:S(2)}) async-start(bf16[192,24,32]{0,1,2:T(8,128)(2,1)} %reshape.56), calls=%async_computation.3 | async-start | bytes 786432 | tf_op jit(solution)/shard_map/all_to_all | solution.py:39
  38.6 0.8 reshape.58
  40.0 1.2 %reshape.55 = bf16[192,24,32]{0,1,2:T(8,128)(2,1)} reshape(bf16[4,48,24,32]{1,0,2,3:T(4,128)(2,1)S(1)} %copy.113) | data formatting | bytes 589824 | tf_op jit(solution)/shard_map/all_to_all | solution.py:47
  41.2 4.9 %all-to-all-done.3 = bf16[192,24,32]{0,1,2:T(8,128)(2,1)S(1)} async-done(((bf16[192,24,32]{0,1,2:T(8,128)(2,1)}), bf16[192,24,32]{0,1,2:T(8,128)(2,1)S(1)}, u32[]{:S(2)}, u32[]{:S(2)}) %all-to-all-start.3) | async-done | bytes 294944 | tf_op jit(solution)/shard_map/all_to_all | solution.py:39
  46.0 3.5 %all-to-all-start.1 = ((bf16[192,24,32]{0,1,2:T(8,128)(2,1)}), bf16[192,24,32]{0,1,2:T(8,128)(2,1)S(1)}, u32[]{:S(2)}, u32[]{:S(2)}) async-start(bf16[192,24,32]{0,1,2:T(8,128)(2,1)} %reshape.55), calls=%async_computation.1 | async-start | bytes 786432 | tf_op jit(solution)/shard_map/all_to_all | solution.py:46
  49.5 7.3 %all-to-all-done.1 = bf16[192,24,32]{0,1,2:T(8,128)(2,1)S(1)} async-done(((bf16[192,24,32]{0,1,2:T(8,128)(2,1)}), bf16[192,24,32]{0,1,2:T(8,128)(2,1)S(1)}, u32[]{:S(2)}, u32[]{:S(2)}) %all-to-all-start.1) | async-done | bytes 294944 | tf_op jit(solution)/shard_map/all_to_all | solution.py:46
  57.5 14.1 %all_to_all.99 = bf16[192,192,4]{1,2,0:T(4,128)(2,1)S(1)} all-to-all(bf16[192,192,4]{1,2,0:T(4,128)(2,1)S(1)} %copy.100), channel_id=1, replica_groups=mesh['row'=4,'col'=2,'depth'=4] {'row'}, dimensions={0} | all-to-all | bytes 589824 | tf_op jit(solution)/shard_map/all_to_all | solution.py:56
  71.8 0.7 copy.103
  72.4 1.9 %reshape.61 = bf16[8,2,9216]{2,1,0:T(2,128)(2,1)} reshape(bf16[192,16,48]{2,1,0:T(8,128)(2,1)S(1)} %bitcast.76) | data formatting | bytes 589824
  74.3 3.6 %all-to-all-start.5 = ((bf16[8,2,9216]{2,1,0:T(2,128)(2,1)}), bf16[8,2,9216]{2,1,0:T(2,128)(2,1)S(1)}, u32[]{:S(2)}, u32[]{:S(2)}) async-start(bf16[8,2,9216]{2,1,0:T(2,128)(2,1)} %reshape.61), calls=%async_computation.5 | async-start | bytes 589824 | tf_op jit(solution)/shard_map/all_to_all | solution.py:55
  79.1 4.9 %all-to-all-done.5 = bf16[8,2,9216]{2,1,0:T(2,128)(2,1)S(1)} async-done(((bf16[8,2,9216]{2,1,0:T(2,128)(2,1)}), bf16[8,2,9216]{2,1,0:T(2,128)(2,1)S(1)}, u32[]{:S(2)}, u32[]{:S(2)}) %all-to-all-start.5) | async-done | bytes 294944 | tf_op jit(solution)/shard_map/all_to_all | solution.py:55
  84.1 0.8 reshape.62
  86.3 1.0 %fusion.11 = bf16[48,24,128]{2,1,0:T(8,128)(2,1)} fusion(f32[48,24,128]{2,1,0:T(8,128)S(1)} %fusion.10, bf16[48,24,128]{2,1,0:T(8,128)(2,1)S(1)} %copy.110, bf16[128,128,1]{1,0,2:T(8,128)(2,1)S(1)} %bitcast.86), kind=kOutput, calls=%fused_computation.15 | convolution fusion | flops 38043648 | bytes 1212416 | tf_op jit(solution)/shard_map/xyc,cd->xyd/dot_general | solution.py:70
  (48 shorter events, 6.0 us)
Async XLA Ops:
  0.0 2.9 %copy-start = (bf16[128,512]{1,0:T(8,128)(2,1)S(1)}, bf16[128,512]{1,0:T(8,128)(2,1)}, u32[]{:S(2)}) copy-start(bf16[128,512]{1,0:T(8,128)(2,1)} %param.11) | copy-start | bytes 393220
  7.3 16.0 %all-to-all-start.2 = ((bf16[4,2,18432]{2,1,0:T(2,128)(2,1)}), bf16[4,2,18432]{2,1,0:T(2,128)(2,1)S(1)}, u32[]{:S(2)}, u32[]{:S(2)}) async-start(bf16[4,2,18432]{2,1,0:T(2,128)(2,1)} %reshape.59), calls=%async_computation.2 | async-start | bytes 589824 | tf_op jit(solution)/shard_map/all_to_all | solution.py:40
  23.3 11.6 %all-to-all-start = ((bf16[4,2,18432]{2,1,0:T(2,128)(2,1)}), bf16[4,2,18432]{2,1,0:T(2,128)(2,1)S(1)}, u32[]{:S(2)}, u32[]{:S(2)}) async-start(bf16[4,2,18432]{2,1,0:T(2,128)(2,1)} %reshape.57), calls=%async_computation | async-start | bytes 589824 | tf_op jit(solution)/shard_map/all_to_all | solution.py:47
  34.9 11.2 %all-to-all-start.3 = ((bf16[192,24,32]{0,1,2:T(8,128)(2,1)}), bf16[192,24,32]{0,1,2:T(8,128)(2,1)S(1)}, u32[]{:S(2)}, u32[]{:S(2)}) async-start(bf16[192,24,32]{0,1,2:T(8,128)(2,1)} %reshape.56), calls=%async_computation.3 | async-start | bytes 786432 | tf_op jit(solution)/shard_map/all_to_all | solution.py:39
  46.0 10.8 %all-to-all-start.1 = ((bf16[192,24,32]{0,1,2:T(8,128)(2,1)}), bf16[192,24,32]{0,1,2:T(8,128)(2,1)S(1)}, u32[]{:S(2)}, u32[]{:S(2)}) async-start(bf16[192,24,32]{0,1,2:T(8,128)(2,1)} %reshape.55), calls=%async_computation.1 | async-start | bytes 786432 | tf_op jit(solution)/shard_map/all_to_all | solution.py:46
  71.7 6.3 %copy-start.5 = (f32[128]{0:T(128)S(1)}, f32[128]{0:T(128)}, u32[]{:S(2)}) copy-start(f32[128]{0:T(128)} %param.13) | copy-start | bytes 1540
  71.7 6.5 %copy-start.6 = (f32[128]{0:T(128)S(1)}, f32[128]{0:T(128)}, u32[]{:S(2)}) copy-start(f32[128]{0:T(128)} %param.14) | copy-start | bytes 1540
  71.7 6.8 %copy-start.2 = (bf16[128,128]{1,0:T(8,128)(2,1)S(1)}, bf16[128,128]{1,0:T(8,128)(2,1)}, u32[]{:S(2)}) copy-start(bf16[128,128]{1,0:T(8,128)(2,1)} %param.15) | copy-start | bytes 98308
  71.7 6.8 %copy-start.1 = (bf16[48,24,128]{2,1,0:T(8,128)(2,1)S(1)}, bf16[48,24,128]{2,1,0:T(8,128)(2,1)}, u32[]{:S(2)}) copy-start(bf16[48,24,128]{2,1,0:T(8,128)(2,1)} %param.8) | copy-start | bytes 884740
  71.7 6.8 %copy-start.3 = (f32[128]{0:T(128)S(1)}, f32[128]{0:T(128)}, u32[]{:S(2)}) copy-start(f32[128]{0:T(128)} %param.10) | copy-start | bytes 1540
  71.7 6.8 %copy-start.4 = (f32[128]{0:T(128)S(1)}, f32[128]{0:T(128)}, u32[]{:S(2)}) copy-start(f32[128]{0:T(128)} %param.9) | copy-start | bytes 1540
  71.7 6.8 %copy-start.7 = (bf16[128,128]{1,0:T(8,128)(2,1)S(1)}, bf16[128,128]{1,0:T(8,128)(2,1)}, u32[]{:S(2)}) copy-start(bf16[128,128]{1,0:T(8,128)(2,1)} %param.12) | copy-start | bytes 98308
  74.3 9.7 %all-to-all-start.5 = ((bf16[8,2,9216]{2,1,0:T(2,128)(2,1)}), bf16[8,2,9216]{2,1,0:T(2,128)(2,1)S(1)}, u32[]{:S(2)}, u32[]{:S(2)}) async-start(bf16[8,2,9216]{2,1,0:T(2,128)(2,1)} %reshape.61), calls=%async_computation.5 | async-start | bytes 589824 | tf_op jit(solution)/shard_map/all_to_all | solution.py:55
where the time goes:
time: 88 us; the launch traced here: 87.3 us
  waiting for transfers between devices  29.8 us (34%)
  starting transfers between devices  20.6 us (23%)
  local copies, waits for them, and re-layouts  15.3 us (17%)
  blocking collectives  14.1 us (16%)
  other arithmetic  3.81 us (4%)
  matrix products  3.41 us (4%)
    all_to_all x1, blocking collectives, per_device(): lax.all_to_all(planes.astype(jnp.bfloat16), 'row', split_axis=0, concat_a...  14.1 us
    unnamed x22, local copies, waits for them, and re-layouts  8.3 us
    all_to_all x1, waiting for transfers between devices, per_device(): lax.all_to_all(lax.all_to_all(right_side, 'row', split_axis=2, concat_axi...  7.34 us
    all_to_all x1, waiting for transfers between devices, per_device(): lax.all_to_all(left_side, 'row', split_axis=2, concat_axis=0, tiled=True)  7.1 us
    all_to_all x1, starting transfers between devices, per_device(): lax.all_to_all(left_side, 'row', split_axis=2, concat_axis=0, tiled=True)  6.35 us
    all_to_all x1, waiting for transfers between devices, per_device(): lax.all_to_all(right_side, 'row', split_axis=2, concat_axis=0, tiled=True)  5.54 us
    all_to_all x1, waiting for transfers between devices, per_device(): lax.all_to_all(lax.all_to_all(planes.astype(jnp.bfloat16), 'row', split_a...  4.94 us
    all_to_all x1, waiting for transfers between devices, per_device(): lax.all_to_all(lax.all_to_all(left_side, 'row', split_axis=2, concat_axis...  4.88 us
  transfers between devices with their start and end apart: 5, of which 5 were waited for; matrix products, arithmetic and copies ran while one was open for 10% of the time, Pallas kernels for 0%

commit v1 on v0

v1 whole, which is shorter than its diff:
```python
import functools

import jax
import jax.numpy as jnp
from jax import lax
from jax.experimental import pallas as pl
from jax.experimental.pallas import tpu as pltpu
from jax.sharding import PartitionSpec as P

F32 = jnp.float32
BF16 = jnp.bfloat16
LANES = 128
SUB = 8


def dot(a, b, ca, cb):
    return lax.dot_general(a, b, (((ca,), (cb,)), ((), ())), preferred_element_type=F32)


def kernel(
    sizes,
    x_ref,
    in_gain_ref,
    in_shift_ref,
    w_proj_ref,
    w_gate_ref,
    out_gain_ref,
    out_shift_ref,
    w_out_ref,
    out_ref,
    normed,
    w_turned,
    gating,
    packed,
    send1,
    recv1,
    gathered,
    left_wide,
    right_wide,
    planes,
    flat,
    packed2,
    send2,
    recv2,
    gathered2,
    send_sem1,
    recv_sem1,
    send_sem2,
    recv_sem2,
):
    rows, cols, depths = sizes
    others = cols * depths
    count = rows * others
    local_k, local_i, width = x_ref.shape
    hidden = w_out_ref.shape[0]
    own = hidden // count
    groups = local_i // SUB
    blocks = local_k // local_i
    pairs = blocks // 2
    tiles = pairs * groups * groups
    span1 = 2 * own * tiles
    padded = packed2.shape[0] // hidden
    span2 = own * padded
    line = groups * others

    my_row = lax.axis_index("row")
    my_other = lax.axis_index("col") * depths + lax.axis_index("depth")
    me = my_row * others + my_other

    def device(p):
        q = lax.rem(p, others)
        return (lax.div(p, others), lax.div(q, depths), lax.rem(q, depths))

    barrier = pltpu.get_barrier_semaphore()

    def greet(d, carry):
        pl.semaphore_signal(
            barrier, inc=1, device_id=device(lax.rem(me + d, count)), device_id_type=pl.DeviceIdType.MESH
        )
        return carry

    lax.fori_loop(1, count, greet, 0)

    values = x_ref[...].astype(F32)
    centred = values - jnp.mean(values, axis=-1, keepdims=True)
    variance = jnp.mean(centred * centred, axis=-1, keepdims=True)
    normed[...] = (
        centred * lax.rsqrt(variance + 1e-05) * in_gain_ref[...].reshape(1, 1, width)
        + in_shift_ref[...].reshape(1, 1, width)
    )
    w_turned[...] = w_proj_ref[...].astype(F32).T.astype(BF16)

    def tile_parts(t):
        pair, rest = t // (groups * groups), t % (groups * groups)
        return pair, rest // groups, rest % groups

    for t in range(tiles):
        pair, first, second = tile_parts(t)
        parts = [
            normed[
                pl.ds((2 * pair + b) * local_i + first * SUB, SUB), pl.ds(second * SUB, SUB), :
            ].reshape(SUB * SUB, width)
            for b in range(2)
        ]
        block = jnp.concatenate(parts, axis=0).astype(BF16)
        projected = dot(w_turned[...], block, 1, 1)
        for side in range(2):
            start = 2 * side * hidden
            gated = (
                jax.nn.sigmoid(projected[start : start + hidden])
                * projected[start + hidden : start + 2 * hidden]
            )
            packed[pl.ds(side * tiles + t, hidden, stride=2 * tiles), :] = gated
        gating[t] = jax.nn.sigmoid(dot(block, w_gate_ref[...], 1, 0))

    def pack1(p, carry):
        send1[p] = packed[pl.ds(pl.multiple_of(p * span1, SUB), span1), :].astype(BF16)
        return carry

    lax.fori_loop(0, count, pack1, 0)
    pl.semaphore_wait(barrier, count - 1)

    def copy1(p, slot):
        return pltpu.make_async_remote_copy(
            src_ref=send1.at[p],
            dst_ref=recv1.at[slot],
            send_sem=send_sem1.at[p],
            recv_sem=recv_sem1.at[slot],
            device_id=device(p),
            device_id_type=pl.DeviceIdType.MESH,
        )

    def copy2(p, slot):
        return pltpu.make_async_remote_copy(
            src_ref=send2.at[p],
            dst_ref=recv2.at[slot],
            send_sem=send_sem2.at[p],
            recv_sem=recv_sem2.at[slot],
            device_id=device(p),
            device_id_type=pl.DeviceIdType.MESH,
        )

    def start1(d, carry):
        copy1(lax.rem(me + d, count), me).start()
        return carry

    lax.fori_loop(1, count, start1, 0)

    gathered[pl.ds(pl.multiple_of(me * span1, SUB), span1), :] = send1[me].astype(F32)

    def take1(d, carry):
        p = lax.rem(me + count - d, count)
        copy1(p, p).wait_recv()
        gathered[pl.ds(pl.multiple_of(p * span1, SUB), span1), :] = recv1[p].astype(F32)
        return carry

    lax.fori_loop(1, count, take1, 0)

    lane_row = lax.broadcasted_iota(jnp.int32, (LANES, LANES), 0)
    lane_col = lax.broadcasted_iota(jnp.int32, (LANES, LANES), 1)
    same_k = lane_row // SUB == lane_col // SUB
    spread = jnp.concatenate(
        [jnp.where(same_k & (lane_row % SUB == j), 1.0, 0.0) for j in range(SUB)], axis=1
    ).astype(BF16)
    lane_of = lax.broadcasted_iota(jnp.int32, (line, LANES), 1)
    zero = jnp.zeros((line, LANES), F32)
    total = SUB * line
    for c in range(own):

        def fill(step, carry, c=c):
            r = lax.div(step, pairs * groups)
            part = lax.rem(step, pairs * groups)

            def side_block(side):
                start = r * others * span1 + (c * 2 + side) * tiles + part * groups
                return jnp.concatenate(
                    [gathered[pl.ds(start + g, others, stride=span1), :] for g in range(groups)], axis=0
                )

            left = side_block(0)
            right = dot(side_block(1).astype(BF16), spread, 1, 0)
            lanes = pl.ds(pl.multiple_of(step * LANES, LANES), LANES)
            left_wide[:, lanes] = jnp.concatenate(
                [jnp.where(lane_of % SUB == i, left, zero) for i in range(SUB)], axis=0
            ).astype(BF16)
            right_wide[:, lanes] = jnp.concatenate(
                [right[:, j * LANES : (j + 1) * LANES] for j in range(SUB)], axis=0
            ).astype(BF16)
            return carry

        lax.fori_loop(0, rows * pairs * groups, fill, 0, unroll=rows * pairs * groups <= 16)
        planes[pl.ds(c * total, total), :] = dot(left_wide[...], right_wide[...], 1, 1).astype(BF16)

    row_of = lax.broadcasted_iota(jnp.int32, (total, LANES), 0)
    col_of = lax.broadcasted_iota(jnp.int32, (total, LANES), 1)
    same_j = row_of // line == col_of % SUB
    row_group = row_of % line

    def flatten(g, carry):
        picker = jnp.where(same_j & (row_group == g), 1.0, 0.0).astype(BF16)
        for c in range(own):
            wide = dot(planes[pl.ds(c * total, total), :], picker, 1, 0)
            kept = wide[:line]
            for i in range(1, SUB):
                kept = jnp.where((lane_of // SUB) % SUB == i, wide[i * line : (i + 1) * line], kept)
            flat[pl.ds(pl.multiple_of((c * line + g) * line, SUB), line), :] = kept
        return carry

    lax.fori_loop(0, line, flatten, 0, unroll=2)

    lane_half = lax.broadcasted_iota(jnp.int32, (others, LANES), 1) < LANES // 2
    for c in range(own):
        for t in range(tiles):
            pair, first, second = tile_parts(t)
            for r in range(rows):
                start = (c * line + second * others) * line + first * others + r * blocks + 2 * pair
                even = flat[pl.ds(start, others, stride=line), :]
                odd = flat[pl.ds(start + 1, others, stride=line), :]
                packed2[pl.ds(r * others * span2 + c * padded + t, others, stride=span2), :] = jnp.where(
                    lane_half, even, odd
                )

    def pack2(p, carry):
        send2[p] = packed2[pl.ds(pl.multiple_of(p * span2, SUB), span2), :].astype(BF16)
        return carry

    lax.fori_loop(0, count, pack2, 0)

    def start2(d, carry):
        copy2(lax.rem(me + d, count), me).start()
        return carry

    lax.fori_loop(1, count, start2, 0)
    out_gain = jnp.broadcast_to(out_gain_ref[...].reshape(1, hidden), (LANES, hidden)).T
    out_shift = jnp.broadcast_to(out_shift_ref[...].reshape(1, hidden), (LANES, hidden)).T
    gathered2[pl.ds(pl.multiple_of(me * span2, SUB), span2), :] = send2[me].astype(F32)

    def take2(d, carry):
        p = lax.rem(me + count - d, count)
        copy2(p, p).wait_recv()
        gathered2[pl.ds(pl.multiple_of(p * span2, SUB), span2), :] = recv2[p].astype(F32)
        return carry

    lax.fori_loop(1, count, take2, 0)

    for t in range(tiles):
        pair, first, second = tile_parts(t)
        product = gathered2[pl.ds(t, hidden, stride=padded), :]
        spread_out = product - jnp.mean(product, axis=0, keepdims=True)
        moment = jnp.mean(spread_out * spread_out, axis=0, keepdims=True)
        product_norm = (spread_out * lax.rsqrt(moment + 1e-05) * out_gain + out_shift).astype(BF16)
        update = (gating[t] * dot(product_norm, w_out_ref[...], 0, 0)).astype(BF16)
        for b in range(2):
            out_ref[
                pl.ds((2 * pair + b) * local_i + first * SUB, SUB), pl.ds(second * SUB, SUB), :
            ] = update[b * SUB * SUB : (b + 1) * SUB * SUB].reshape(SUB, SUB, width)

    def finish(d, carry):
        p = lax.rem(me + d, count)
        copy1(p, me).wait_send()
        copy2(p, me).wait_send()
        return carry

    lax.fori_loop(1, count, finish, 0)


def per_device(sizes, pair_input, in_gain, in_shift, w_proj, w_gate, out_gain, out_shift, w_out):
    rows, cols, depths = sizes
    others = cols * depths
    count = rows * others
    local_k, local_i, width = pair_input.shape
    hidden = w_out.shape[0]
    own = hidden // count
    residues = local_k * rows
    tiles = local_k * local_i // LANES
    span1 = 2 * own * tiles
    padded = tiles
    while (own * padded) % SUB:
        padded += 1
    span2 = own * padded
    line = residues // SUB
    deep = residues * SUB
    vmem = pl.BlockSpec(memory_space=pltpu.VMEM)
    return pl.pallas_call(
        functools.partial(kernel, sizes),
        out_shape=jax.ShapeDtypeStruct(pair_input.shape, BF16),
        in_specs=[vmem] * 8,
        out_specs=vmem,
        scratch_shapes=[
            pltpu.VMEM(pair_input.shape, F32),
            pltpu.VMEM(w_proj.shape[::-1], BF16),
            pltpu.VMEM((tiles, LANES, width), F32),
            pltpu.VMEM((hidden * 2 * tiles, LANES), F32),
            pltpu.VMEM((count, span1, LANES), BF16),
            pltpu.VMEM((count, span1, LANES), BF16),
            pltpu.VMEM((count * span1, LANES), F32),
            pltpu.VMEM((residues, deep), BF16),
            pltpu.VMEM((residues, deep), BF16),
            pltpu.VMEM((own * residues, residues), BF16),
            pltpu.VMEM((own * line * line, LANES), F32),
            pltpu.VMEM((hidden * padded, LANES), F32),
            pltpu.VMEM((count, span2, LANES), BF16),
            pltpu.VMEM((count, span2, LANES), BF16),
            pltpu.VMEM((hidden * padded, LANES), F32),
            pltpu.SemaphoreType.DMA((count,)),
            pltpu.SemaphoreType.DMA((count,)),
            pltpu.SemaphoreType.DMA((count,)),
            pltpu.SemaphoreType.DMA((count,)),
        ],
        compiler_params=pltpu.CompilerParams(
            collective_id=0, has_side_effects=True, vmem_limit_bytes=60 * 1024 * 1024
        ),
    )(
        pair_input,
        in_gain.reshape(1, -1),
        in_shift.reshape(1, -1),
        w_proj,
        w_gate,
        out_gain.reshape(1, -1),
        out_shift.reshape(1, -1),
        w_out,
    )


def solution(mesh):
    sizes = (mesh.shape["row"], mesh.shape["col"], mesh.shape["depth"])
    placed = (P("row", ("col", "depth"), None), P(), P(), P(), P(), P(), P(), P())
    return jax.shard_map(
        functools.partial(per_device, sizes),
        mesh=mesh,
        in_specs=placed,
        out_specs=P("row", ("col", "depth"), None),
        check_vma=False,
    )
```

time: 88 us -> 40.9 us (0.46)
  Pallas kernels: 0 us -> 38.8 us
  waiting for transfers between devices: 29.8 us -> 0 us
  starting transfers between devices: 20.6 us -> 0 us
  blocking collectives: 14.1 us -> 0 us
  local copies, waits for them, and re-layouts: 15.3 us -> 1.71 us
  other arithmetic: 3.81 us -> 0 us
  matrix products: 3.41 us -> 0 us
    pallas_call x0 -> x1, Pallas kernels: none -> 38.8 us  [per_device(): pl.pallas_call(functools.partial(kernel, sizes), out_shape=jax.ShapeDtype...]
    all_to_all x5 -> x0, waiting for transfers between devices: 29.8 us -> none  [the longest x1 7.34 us: per_device(): lax.all_to_all(lax.all_to_all(right_side, 'row', split_axis=2, concat_axi...]
    all_to_all x5 -> x0, starting transfers between devices: 20.6 us -> none  [the longest x1 6.35 us: per_device(): lax.all_to_all(left_side, 'row', split_axis=2, concat_axis=0, tiled=True)]
    all_to_all x1 -> x0, blocking collectives: 14.1 us -> none  [per_device(): lax.all_to_all(planes.astype(jnp.bfloat16), 'row', split_axis=0, concat_a...]
    unnamed x22 -> x1, local copies, waits for them, and re-layouts: 8.3 us -> 1.71 us
    all_to_all x9 -> x0, local copies, waits for them, and re-layouts: 4.36 us -> none  [the longest x2 1.8 us: per_device(): lax.all_to_all(left_side, 'row', split_axis=2, concat_axis=0, tiled=True)]
    dot_general x4 -> x0, matrix products: 3.41 us -> none  [the longest x1 1.56 us: gated_sides(): jnp.einsum('xyc,cd->xyd', normed, w_proj, preferred_element_type=jnp.floa...]
    reduce_sum x4 -> x0, other arithmetic: 3.05 us -> none  [the longest x2 1.65 us: layer_norm(): variance = jnp.mean(centred * centred, axis=-1, keepdims=True)]
  transfers between devices with their start and end apart: 5 -> 0, of which waited for: 5 -> 0; matrix products, arithmetic and copies ran while one was open for 10% -> 0% of each run, Pallas kernels for 0% -> 0%
where the time goes in v1:
time: 40.9 us; the launch traced here: 40.5 us
  Pallas kernels  38.8 us (95%)
  local copies, waits for them, and re-layouts  1.71 us (4%)
    pallas_call x1, Pallas kernels, per_device(): pl.pallas_call(functools.partial(kernel, sizes), out_shape=jax.ShapeDtype...  38.8 us
    unnamed x1, local copies, waits for them, and re-layouts  1.71 us

profile of v1, /device:TPU:0, one launch (start us, length us, event | category | flops | bytes accessed | tf_op | source)
XLA Modules:
  0.0 40.5 jit_solution(4437725190873774775)
XLA Ops:
  0.0 38.8 %shard_map.82 = bf16[48,24,128]{2,1,0:T(8,128)(2,1)} custom-call(bf16[48,24,128]{2,1,0:T(8,128)(2,1)} %x_ref.1, f32[1,128]{1,0:T(1,128)} %bitcast.4, f32[1,128]{1,0:T(1,128)} %bitcast.5, bf16[128,512]{1,0:T(8,128)(2,1)} %w_proj_ref.1, bf16[128,128]{1,0:T(8,128)(2,1)} %w_gate_ref.1, f32[1,128]{1,0:T(1,128)} %bitcast.6, f32[1,128]{1,0:T(1,128)} %bitcast.7, ...), custom_call_target="tpu_custom_call" | custom-call | tf_op jit(solution)/shard_map/pallas_call | solution.py:284
  38.8 1.7 %copy.10 = bf16[48,24,128]{2,1,0:T(8,128)(2,1)} copy(bf16[48,24,128]{2,1,0:T(8,128)(2,1)} %shard_map.82) | data formatting | bytes 589824

commit v2 on v1

v2 whole, which is shorter than its diff:
```python
import functools

import jax
import jax.numpy as jnp
from jax import lax
from jax.experimental import pallas as pl
from jax.experimental.pallas import tpu as pltpu
from jax.sharding import PartitionSpec as P

F32 = jnp.float32
BF16 = jnp.bfloat16
LANES = 128
SUB = 8
HALVES = 1


def padded_rows(needed, channels):
    while (needed * channels) % SUB:
        needed += 1
    return needed


def dot(a, b, ca, cb):
    return lax.dot_general(a, b, (((ca,), (cb,)), ((), ())), preferred_element_type=F32)


def kernel(
    sizes,
    x_ref,
    in_gain_ref,
    in_shift_ref,
    w_proj_ref,
    w_gate_ref,
    out_gain_ref,
    out_shift_ref,
    w_out_ref,
    out_ref,
    normed,
    w_turned,
    gating,
    packed,
    send1,
    recv1,
    gathered,
    left_wide,
    right_wide,
    planes,
    flat,
    packed2,
    send2,
    recv2,
    gathered2,
    spread,
    picker,
    send_sem1,
    recv_sem1,
    send_sem2,
    recv_sem2,
):
    rows, cols, depths = sizes
    others = cols * depths
    count = rows * others
    local_k, local_i, width = x_ref.shape
    hidden = w_out_ref.shape[0]
    own = hidden // count
    groups = local_i // SUB
    blocks = local_k // local_i
    pairs = blocks // 2
    tiles = pairs * groups * groups
    halves = send1.shape[0]
    own_half = own // halves
    part_hidden = hidden // halves
    padded1 = packed.shape[0] // hidden
    padded2 = packed2.shape[0] // hidden
    span1 = own_half * padded1
    span2 = own_half * padded2
    line = groups * others

    my_row = lax.axis_index("row")
    my_other = lax.axis_index("col") * depths + lax.axis_index("depth")
    me = my_row * others + my_other

    def device(p):
        q = lax.rem(p, others)
        return (lax.div(p, others), lax.div(q, depths), lax.rem(q, depths))

    barrier = pltpu.get_barrier_semaphore()

    def greet(d, carry):
        pl.semaphore_signal(
            barrier, inc=1, device_id=device(lax.rem(me + d, count)), device_id_type=pl.DeviceIdType.MESH
        )
        return carry

    lax.fori_loop(1, count, greet, 0)

    values = x_ref[...].astype(F32)
    centred = values - jnp.mean(values, axis=-1, keepdims=True)
    variance = jnp.mean(centred * centred, axis=-1, keepdims=True)
    normed[...] = (
        centred * lax.rsqrt(variance + 1e-05) * in_gain_ref[...].reshape(1, 1, width)
        + in_shift_ref[...].reshape(1, 1, width)
    )
    w_turned[...] = w_proj_ref[...].astype(F32).T.astype(BF16)

    def tile_parts(t):
        pair, rest = t // (groups * groups), t % (groups * groups)
        return pair, rest // groups, rest % groups

    def tile_block(t):
        pair, first, second = tile_parts(t)
        parts = [
            normed[
                pl.ds((2 * pair + b) * local_i + first * SUB, SUB), pl.ds(second * SUB, SUB), :
            ].reshape(SUB * SUB, width)
            for b in range(2)
        ]
        return jnp.concatenate(parts, axis=0).astype(BF16)

    def project(h):
        for t in range(tiles):
            block = tile_block(t)
            for side in range(2):
                start = 2 * side * hidden + h * part_hidden
                gates = dot(w_turned[pl.ds(start, part_hidden), :], block, 1, 1)
                edges = dot(w_turned[pl.ds(start + hidden, part_hidden), :], block, 1, 1)
                packed[
                    pl.ds(h * part_hidden * padded1 + side * tiles + t, part_hidden, stride=padded1), :
                ] = jax.nn.sigmoid(gates) * edges

        def pack1(p, carry):
            start = pl.multiple_of((h * count + p) * span1, SUB)
            send1[h, p] = packed[pl.ds(start, span1), :].astype(BF16)
            return carry

        lax.fori_loop(0, count, pack1, 0, unroll=4)

    def copy1(h, p, slot):
        return pltpu.make_async_remote_copy(
            src_ref=send1.at[h, p],
            dst_ref=recv1.at[h, slot],
            send_sem=send_sem1.at[h, p],
            recv_sem=recv_sem1.at[h, slot],
            device_id=device(p),
            device_id_type=pl.DeviceIdType.MESH,
        )

    def copy2(h, p, slot):
        return pltpu.make_async_remote_copy(
            src_ref=send2.at[h, p],
            dst_ref=recv2.at[h, slot],
            send_sem=send_sem2.at[h, p],
            recv_sem=recv_sem2.at[h, slot],
            device_id=device(p),
            device_id_type=pl.DeviceIdType.MESH,
        )

    def peer(d):
        return lax.rem(me + d, count)

    for h in range(halves):
        project(h)
        if h == 0:
            pl.semaphore_wait(barrier, count - 1)

        def start1(d, carry, h=h):
            copy1(h, peer(d), me).start()
            return carry

        lax.fori_loop(1, count, start1, 0)

    for t in range(tiles):
        gating[t] = jax.nn.sigmoid(dot(tile_block(t), w_gate_ref[...], 1, 0))
    lane_row = lax.broadcasted_iota(jnp.int32, (LANES, LANES), 0)
    lane_col = lax.broadcasted_iota(jnp.int32, (LANES, LANES), 1)
    same_k = lane_row // SUB == lane_col // SUB
    for j in range(SUB):
        spread[:, j * LANES : (j + 1) * LANES] = jnp.where(
            same_k & (lane_row % SUB == j), 1.0, 0.0
        ).astype(BF16)
    total = SUB * line
    row_of = lax.broadcasted_iota(jnp.int32, (total, 2 * LANES), 0)
    col_of = lax.broadcasted_iota(jnp.int32, (total, 2 * LANES), 1)
    same_j = row_of // line == col_of % SUB
    row_group = row_of % line
    half_line = others // 2
    second_half = jnp.where(col_of % LANES < LANES // 2, 0, half_line)
    hoisted = picker.shape[0] == line // 4

    def group_of(pair):
        return lax.div(pair, half_line) * others + lax.rem(pair, half_line)

    def fill_picker(g, slot):
        wanted = jnp.where(col_of < LANES, group_of(2 * g), group_of(2 * g + 1)) + second_half
        picker[slot] = jnp.where(same_j & (row_group == wanted), 1.0, 0.0).astype(BF16)

    if hoisted:

        def hoist(g, carry):
            fill_picker(g, g)
            return carry

        lax.fori_loop(0, line // 4, hoist, 0)
    lane_of = lax.broadcasted_iota(jnp.int32, (line, LANES), 1)
    lane_half = lax.broadcasted_iota(jnp.int32, (others, LANES), 1) < LANES // 2
    zero = jnp.zeros((line, LANES), F32)
    wide_of = lax.broadcasted_iota(jnp.int32, (line, 2 * LANES), 1)
    odd_row = lax.broadcasted_iota(jnp.int32, (line, LANES), 0) % 2 == 1
    steps = rows * pairs * groups
    batch = max(n for n in range(1, steps + 1) if steps % n == 0 and (n * line <= 288 or n == 1))

    def middle(h):
        base = h * count * span1
        start = pl.multiple_of(base + me * span1, SUB)
        gathered[pl.ds(start, span1), :] = send1[h, me].astype(F32)

        def take1(d, carry):
            p = lax.rem(me + count - d, count)
            copy1(h, p, p).wait_recv()
            start = pl.multiple_of(base + p * span1, SUB)
            gathered[pl.ds(start, span1), :] = recv1[h, p].astype(F32)
            return carry

        lax.fori_loop(1, count, take1, 0)
        for c in range(own_half):

            def fill(turn, carry, c=c):
                rights = []
                for n in range(batch):
                    step = turn * batch + n
                    r = lax.div(step, pairs * groups)
                    part = lax.rem(step, pairs * groups)
                    start = base + r * others * span1 + c * padded1 + part * groups
                    left = jnp.concatenate(
                        [gathered[pl.ds(start + g, others, stride=span1), :] for g in range(groups)],
                        axis=0,
                    )
                    rights += [
                        gathered[pl.ds(start + tiles + g, others, stride=span1), :]
                        for g in range(groups)
                    ]
                    lanes = pl.ds(pl.multiple_of(step * LANES, LANES), LANES)
                    left_wide[:, lanes] = jnp.concatenate(
                        [jnp.where(lane_of % SUB == i, left, zero) for i in range(SUB)], axis=0
                    ).astype(BF16)
                right = dot(jnp.concatenate(rights, axis=0).astype(BF16), spread[...], 1, 0)
                for n in range(batch):
                    lanes = pl.ds(pl.multiple_of((turn * batch + n) * LANES, LANES), LANES)
                    right_wide[:, lanes] = jnp.concatenate(
                        [
                            right[n * line : (n + 1) * line, j * LANES : (j + 1) * LANES]
                            for j in range(SUB)
                        ],
                        axis=0,
                    ).astype(BF16)
                return carry

            if steps == batch:
                fill(0, 0)
            else:
                lax.fori_loop(0, steps // batch, fill, 0)
            planes[pl.ds(c * total, total), :] = dot(left_wide[...], right_wide[...], 1, 1).astype(BF16)

        def flatten(g, carry):
            slot = g if hoisted else 0
            if not hoisted:
                fill_picker(g, 0)
            for c in range(own_half):
                wide = dot(planes[pl.ds(c * total, total), :], picker[slot], 1, 0)
                kept = wide[:line]
                for i in range(1, SUB):
                    kept = jnp.where((wide_of // SUB) % SUB == i, wide[i * line : (i + 1) * line], kept)
                for n in range(2):
                    mine = kept[:, n * LANES : (n + 1) * LANES]
                    turned = pltpu.roll(mine, LANES // 2, 1)
                    group = group_of(2 * g + n)
                    low = pl.multiple_of((c * line + group) * line, SUB)
                    high = pl.multiple_of((c * line + group + half_line) * line, SUB)
                    flat[pl.ds(low, line), :] = jnp.where(odd_row, turned, mine)
                    flat[pl.ds(high, line), :] = jnp.where(odd_row, mine, turned)
            return carry

        lax.fori_loop(0, line // 4, flatten, 0, unroll=2)
        for c in range(own_half):
            for t in range(tiles):
                pair, first, second = tile_parts(t)
                for r in range(rows):
                    start = (c * line + second * others) * line + first * others + r * blocks + 2 * pair
                    even = flat[pl.ds(start, others, stride=line), :]
                    odd = flat[pl.ds(start + 1, others, stride=line), :]
                    packed2[
                        pl.ds((h * count + r * others) * span2 + c * padded2 + t, others, stride=span2), :
                    ] = jnp.where(lane_half, even, odd)

        def pack2(p, carry):
            start = pl.multiple_of((h * count + p) * span2, SUB)
            send2[h, p] = packed2[pl.ds(start, span2), :].astype(BF16)
            return carry

        lax.fori_loop(0, count, pack2, 0, unroll=4)

        def start2(d, carry):
            copy2(h, peer(d), me).start()
            return carry

        lax.fori_loop(1, count, start2, 0)

    for h in range(halves):
        middle(h)
    out_gain = jnp.broadcast_to(out_gain_ref[...].reshape(1, hidden), (LANES, hidden)).T
    out_shift = jnp.broadcast_to(out_shift_ref[...].reshape(1, hidden), (LANES, hidden)).T
    for h in range(halves):
        start = pl.multiple_of((h * count + me) * span2, SUB)
        gathered2[pl.ds(start, span2), :] = send2[h, me].astype(F32)

        def take2(d, carry, h=h):
            p = lax.rem(me + count - d, count)
            copy2(h, p, p).wait_recv()
            start = pl.multiple_of((h * count + p) * span2, SUB)
            gathered2[pl.ds(start, span2), :] = recv2[h, p].astype(F32)
            return carry

        lax.fori_loop(1, count, take2, 0)

    for t in range(tiles):
        pair, first, second = tile_parts(t)
        product = gathered2[pl.ds(t, hidden, stride=padded2), :]
        spread_out = product - jnp.mean(product, axis=0, keepdims=True)
        moment = jnp.mean(spread_out * spread_out, axis=0, keepdims=True)
        product_norm = (spread_out * lax.rsqrt(moment + 1e-05) * out_gain + out_shift).astype(BF16)
        update = (gating[t] * dot(product_norm, w_out_ref[...], 0, 0)).astype(BF16)
        for b in range(2):
            out_ref[
                pl.ds((2 * pair + b) * local_i + first * SUB, SUB), pl.ds(second * SUB, SUB), :
            ] = update[b * SUB * SUB : (b + 1) * SUB * SUB].reshape(SUB, SUB, width)

    def finish(d, carry):
        p = lax.rem(me + d, count)
        for h in range(halves):
            copy1(h, p, me).wait_send()
            copy2(h, p, me).wait_send()
        return carry

    lax.fori_loop(1, count, finish, 0)


def per_device(sizes, pair_input, in_gain, in_shift, w_proj, w_gate, out_gain, out_shift, w_out):
    rows, cols, depths = sizes
    others = cols * depths
    count = rows * others
    local_k, local_i, width = pair_input.shape
    hidden = w_out.shape[0]
    own = hidden // count
    residues = local_k * rows
    tiles = local_k * local_i // LANES
    halves = HALVES if own % HALVES == 0 else 1
    own_half = own // halves
    padded1 = padded_rows(2 * tiles, own_half)
    padded2 = padded_rows(tiles, own_half)
    span1 = own_half * padded1
    span2 = own_half * padded2
    line = residues // SUB
    deep = residues * SUB
    pickers = line // 4 if residues * line * LANES <= 1 << 20 else 1
    vmem = pl.BlockSpec(memory_space=pltpu.VMEM)
    return pl.pallas_call(
        functools.partial(kernel, sizes),
        out_shape=jax.ShapeDtypeStruct(pair_input.shape, BF16),
        in_specs=[vmem] * 8,
        out_specs=vmem,
        scratch_shapes=[
            pltpu.VMEM(pair_input.shape, F32),
            pltpu.VMEM(w_proj.shape[::-1], BF16),
            pltpu.VMEM((tiles, LANES, width), F32),
            pltpu.VMEM((hidden * padded1, LANES), F32),
            pltpu.VMEM((halves, count, span1, LANES), BF16),
            pltpu.VMEM((halves, count, span1, LANES), BF16),
            pltpu.VMEM((hidden * padded1, LANES), F32),
            pltpu.VMEM((residues, deep), BF16),
            pltpu.VMEM((residues, deep), BF16),
            pltpu.VMEM((own_half * residues, residues), BF16),
            pltpu.VMEM((own_half * line * line, LANES), F32),
            pltpu.VMEM((hidden * padded2, LANES), F32),
            pltpu.VMEM((halves, count, span2, LANES), BF16),
            pltpu.VMEM((halves, count, span2, LANES), BF16),
            pltpu.VMEM((hidden * padded2, LANES), F32),
            pltpu.VMEM((LANES, SUB * LANES), BF16),
            pltpu.VMEM((pickers, residues, 2 * LANES), BF16),
            pltpu.SemaphoreType.DMA((halves, count)),
            pltpu.SemaphoreType.DMA((halves, count)),
            pltpu.SemaphoreType.DMA((halves, count)),
            pltpu.SemaphoreType.DMA((halves, count)),
        ],
        compiler_params=pltpu.CompilerParams(
            collective_id=0, has_side_effects=True, vmem_limit_bytes=67_000_000
        ),
    )(
        pair_input,
        in_gain.reshape(1, -1),
        in_shift.reshape(1, -1),
        w_proj,
        w_gate,
        out_gain.reshape(1, -1),
        out_shift.reshape(1, -1),
        w_out,
    )


def solution(mesh):
    sizes = (mesh.shape["row"], mesh.shape["col"], mesh.shape["depth"])
    placed = (P("row", ("col", "depth"), None), P(), P(), P(), P(), P(), P(), P())
    return jax.shard_map(
        functools.partial(per_device, sizes),
        mesh=mesh,
        in_specs=placed,
        out_specs=P("row", ("col", "depth"), None),
        check_vma=False,
    )
```

time: 40.9 us -> 36.8 us (0.90)
  Pallas kernels: 38.8 us -> 34.8 us
    pallas_call x1, Pallas kernels: 38.8 us -> 34.8 us  [per_device(): pl.pallas_call(functools.partial(kernel, sizes), out_shape=jax.ShapeDtype...]
where the time goes in v2:
time: 36.8 us; the launch traced here: 36.5 us
  Pallas kernels  34.8 us (95%)
  local copies, waits for them, and re-layouts  1.71 us (5%)
    pallas_call x1, Pallas kernels, per_device(): pl.pallas_call(functools.partial(kernel, sizes), out_shape=jax.ShapeDtype...  34.8 us
    unnamed x1, local copies, waits for them, and re-layouts  1.71 us

profile of v2, /device:TPU:0, one launch (start us, length us, event | category | flops | bytes accessed | tf_op | source)
XLA Modules:
  0.0 36.5 jit_solution(17536981643585423784)
XLA Ops:
  0.0 34.8 %shard_map.82 = bf16[48,24,128]{2,1,0:T(8,128)(2,1)} custom-call(bf16[48,24,128]{2,1,0:T(8,128)(2,1)} %x_ref.1, f32[1,128]{1,0:T(1,128)} %bitcast.4, f32[1,128]{1,0:T(1,128)} %bitcast.5, bf16[128,512]{1,0:T(8,128)(2,1)} %w_proj_ref.1, bf16[128,128]{1,0:T(8,128)(2,1)} %w_gate_ref.1, f32[1,128]{1,0:T(1,128)} %bitcast.6, f32[1,128]{1,0:T(1,128)} %bitcast.7, ...), custom_call_target="tpu_custom_call" | custom-call | tf_op jit(solution)/shard_map/pallas_call | solution.py:366
  34.8 1.7 %copy.10 = bf16[48,24,128]{2,1,0:T(8,128)(2,1)} copy(bf16[48,24,128]{2,1,0:T(8,128)(2,1)} %shard_map.82) | data formatting | bytes 589824
